TPU v7x, 32 devices: a whole 2x2x4 slice. The times are simulated.
32 devices in a mesh: py: 4 (over y, x), px: 4 (over z), pz: 2 (over core).
Axes of the slice: x: 2, y: 2, z: 4, core: 2. Of those that a mesh axis runs over, the one named last changes fastest.
Arguments:
- field_now: float32 [16, 512, 64, 128], P('py', 'px', 'pz'), may hold values from 0.5 to 2
- earlier: float32 [16, 512, 64, 128], P('py', 'px', 'pz'), may hold values from 0.2 to 1.8
- speed_square: float32 [16, 512, 64, 128], P('py', 'px', 'pz'), may hold values from 0.05 to 0.3
Outputs:
- anomaly: float32 [16, 512, 64, 128], P('py', 'px', 'pz')
- field_now_end: float32 [16, 512, 64, 128], P('py', 'px', 'pz')
All inputs are finite; a program needn't handle non-finite values.
Results may differ from a plain program's by a relative error of at most 0.00002.
Values sent between devices are 32-bit elements; how exact they have to be, the bound alone decides.
A program may use at most 128 MiB of HBM per device.

v0:
```python
import functools

import jax
import jax.numpy as jnp
from jax import lax
from jax.experimental import pallas as pl
from jax.experimental.pallas import tpu as pltpu
from jax.sharding import PartitionSpec as P

STEPS = 4
PAD = 8
LIMIT = 54 * 2**20
MESH = pl.DeviceIdType.MESH


def relays(mesh):
    devices = mesh.devices
    line = [devices[(n,) + (0,) * (devices.ndim - 1)] for n in range(devices.shape[0])]
    places = [getattr(device, "coords", None) for device in line]
    if any(place is None for place in places):
        return ()
    places = [tuple(place) for place in places]
    jobs = []
    for low in range(len(line) - 1):
        for a, b in ((low, low + 1), (low + 1, low)):
            turn = (places[a][0],) + places[b][1:]
            if turn in places and turn not in (places[a], places[b]):
                jobs.append((a, b, places.index(turn)))
    return tuple(jobs)


def steps_kernel(jobs, pieces, axes, f_ref, e_ref, c_ref, far, mean_out, scale_out,
                 field, speed, halo, relay, stat_in, stat_edge, load_sem, py_send, py_recv,
                 r_send, r_recv, side_send, side_recv, st_send, st_recv):
    planes, lines, depth, levels = c_ref.shape
    tiles = depth // PAD
    chunks = tiles * pieces
    rows = lines // pieces
    edges = sorted({0, planes - 1})
    inner = pl.ds(PAD, depth)
    me = {name: lax.axis_index(name) for name in axes}
    count = {name: axes[name] for name in axes}
    py = me["py"]

    barrier = pltpu.get_barrier_semaphore()
    greeted = 0
    for name in axes:
        for n in range(1, count[name]):
            pl.semaphore_signal(
                barrier, inc=1, device_id={name: lax.rem(me[name] + n, count[name])},
                device_id_type=MESH,
            )
            greeted += 1
    pl.semaphore_wait(barrier, greeted)

    def there(name, way):
        return me[name] < count[name] - 1 if way else me[name] > 0

    def done(ref, sem):
        pltpu.make_async_copy(ref, ref, sem).wait()

    def part(c, line, cell):
        start = cell + (c // pieces) * PAD
        if cell % PAD == 0:
            start = pl.multiple_of(start, PAD)
        return pl.ds(line + (c % pieces) * rows, rows), pl.ds(start, PAD)

    def edge(step, c, way):
        plane = planes - 1 if way else 0
        if step == 0:
            return f_ref.at[(plane,) + part(c, 0, 0)]
        return field.at[(step % 2, plane) + part(c, 1, PAD)]

    def landing(step, c, side):
        return halo.at[(side, step % 2) + part(c, 0, 0)]

    def send_py(step, c):
        for way in (0, 1):
            beyond = py + (2 * way - 1)
            direct = there("py", way)
            for slot, (a, b, via) in enumerate(jobs):
                if b - a != 2 * way - 1:
                    continue
                turned = jnp.logical_and(py == a, c % 2 == 1)
                direct = jnp.logical_and(direct, jnp.logical_not(turned))

                @pl.when(turned)
                def _(slot=slot, via=via, way=way):
                    pltpu.make_async_remote_copy(
                        src_ref=edge(step, c, way),
                        dst_ref=relay.at[job_slot(slot), step, c // 2],
                        send_sem=py_send.at[way, step % 2, c],
                        recv_sem=r_recv.at[job_slot(slot), step, c // 2],
                        device_id={"py": via}, device_id_type=MESH,
                    ).start()

            @pl.when(direct)
            def _(way=way, beyond=beyond):
                pltpu.make_async_remote_copy(
                    src_ref=edge(step, c, way),
                    dst_ref=landing(step, c, 1 - way),
                    send_sem=py_send.at[way, step % 2, c],
                    recv_sem=py_recv.at[1 - way, step % 2, c],
                    device_id={"py": beyond}, device_id_type=MESH,
                ).start()

    def job_slot(slot):
        return [via for _, _, via in jobs[:slot]].count(jobs[slot][2])

    def forward(step, c):
        for slot, (a, b, via) in enumerate(jobs):
            @pl.when(py == via)
            def _(slot=slot, a=a, b=b):
                way = 1 if b > a else 0
                held = relay.at[job_slot(slot), step, c // 2]
                done(held, r_recv.at[job_slot(slot), step, c // 2])
                pltpu.make_async_remote_copy(
                    src_ref=held,
                    dst_ref=landing(step, c, 1 - way),
                    send_sem=r_send.at[job_slot(slot), step, c // 2],
                    recv_sem=py_recv.at[1 - way, step % 2, c],
                    device_id={"py": b}, device_id_type=MESH,
                ).start()

    def forward_late(step, c):
        if jobs:
            @pl.when(jnp.logical_and(c % 2 == 0, c > 0))
            def _():
                forward(step, c - 1)

    def sent_py(step, c):
        for way in (0, 1):
            @pl.when(there("py", way))
            def _(way=way):
                done(edge(step, c, way), py_send.at[way, step % 2, c])

    def arrived_py(step, c):
        for side in (0, 1):
            @pl.when(there("py", side))
            def _(side=side):
                done(landing(step, c, side), py_recv.at[side, step % 2, c])

    def side_source(step, name, way):
        if name == "px":
            at = lines - 1 if way else 0
            if step == 0:
                return f_ref.at[:, pl.ds(at, 1)]
            return field.at[step % 2, :, pl.ds(1 + at, 1), inner]
        at = depth - PAD if way else 0
        if step == 0:
            return f_ref.at[:, :, pl.ds(at, PAD)]
        return field.at[step % 2, :, pl.ds(1, lines), pl.ds(PAD + at, PAD)]

    def side_landing(slot, name, side):
        if name == "px":
            return field.at[slot, :, pl.ds(lines + 1 if side else 0, 1), inner]
        return field.at[slot, :, pl.ds(1, lines), pl.ds(PAD + depth if side else 0, PAD)]

    def sides(step, what):
        for n, name in enumerate(("px", "pz")):
            for way in (0, 1):
                @pl.when(there(name, way))
                def _(n=n, name=name, way=way):
                    if what == "send":
                        pltpu.make_async_remote_copy(
                            src_ref=side_source(step, name, way),
                            dst_ref=side_landing(step % 2, name, 1 - way),
                            send_sem=side_send.at[n, way, step % 2],
                            recv_sem=side_recv.at[n, 1 - way, step % 2],
                            device_id={name: me[name] + (2 * way - 1)}, device_id_type=MESH,
                        ).start()
                    elif what == "sent":
                        done(side_source(step, name, way), side_send.at[n, way, step % 2])
                    else:
                        done(side_landing(step % 2, name, way), side_recv.at[n, way, step % 2])

    whole = lambda slot: field.at[slot, :, pl.ds(1, lines), inner]
    loads = [
        pltpu.make_async_copy(f_ref, whole(0), load_sem.at[0]),
        pltpu.make_async_copy(e_ref, whole(1), load_sem.at[1]),
        pltpu.make_async_copy(c_ref, speed, load_sem.at[2]),
    ]

    def first(c, _):
        send_py(0, c)
        forward_late(0, c)
        return 0

    lax.fori_loop(0, 2, first, 0)
    sides(0, "send")
    for load in loads:
        load.start()
    lax.fori_loop(2, chunks, first, 0)
    forward(0, chunks - 1)

    for way in (0, 1):
        @pl.when(jnp.logical_not(there("py", way)))
        def _(way=way):
            def clear(i, _):
                for slot in (0, 1):
                    halo[way, slot, i] = jnp.zeros((depth, levels), jnp.float32)
                return 0
            lax.fori_loop(0, lines, clear, 0)

        @pl.when(jnp.logical_not(there("px", way)))
        def _(way=way):
            for slot in (0, 1):
                for j in range(planes):
                    field[slot, j, lines + 1 if way else 0, inner, :] = jnp.zeros((depth, levels), jnp.float32)

        @pl.when(jnp.logical_not(there("pz", way)))
        def _(way=way):
            def clear(i, _):
                for slot in (0, 1):
                    for j in range(planes):
                        field[slot, j, 1 + i, pl.ds(PAD + depth if way else 0, PAD), :] = jnp.zeros((PAD, levels), jnp.float32)
                return 0
            lax.fori_loop(0, lines, clear, 0)

    for load in loads:
        load.wait()

    px, blocks = me["px"], count["px"]

    def cells(start, tile):
        start = start + tile * PAD
        return pl.ds(pl.multiple_of(start, PAD) if isinstance(start, jax.Array) and start.ndim == 0 else start, PAD)

    def update(step, which, i, tile):
        now, other = step % 2, (step + 1) % 2
        mid, own = cells(PAD, tile), cells(0, tile)
        for j in which:
            here = field[now, j, i + 1, mid, :]
            below = field[now, j - 1, i + 1, mid, :] if j else halo[0, now, i, own, :]
            above = field[now, j + 1, i + 1, mid, :] if j < planes - 1 else halo[1, now, i, own, :]
            spread = (
                below + above
                + field[now, j, i, mid, :] + field[now, j, i + 2, mid, :]
                + field[now, j, i + 1, pl.ds(PAD - 1 + tile * PAD, PAD), :]
                + field[now, j, i + 1, pl.ds(PAD + 1 + tile * PAD, PAD), :]
                - 6.0 * here
            )
            later = 2.0 * here - field[other, j, i + 1, mid, :] + speed[j, i, own, :] * spread
            if step < STEPS - 1:
                field[other, j, i + 1, mid, :] = later
            else:
                far[j, i, own, :] = later

    def sums(which, tile):
        own = cells(0, tile)
        base = [far[j, 0, own, :] for j in which]

        def add(i, held):
            moved = [far[j, i, own, :] - b for j, b in zip(which, base)]
            return [(t + m, q + m * m) for (t, q), m in zip(held, moved)]

        zero = jnp.zeros((PAD, levels), jnp.float32)
        held = lax.fori_loop(0, lines, add, [(zero, zero) for _ in which], unroll=8)
        return [
            (b + t / lines, jnp.maximum(q - t * (t / lines), 0.0)) for b, (t, q) in zip(base, held)
        ]

    def send_stat(ref, slot):
        for n in range(1, blocks):
            pltpu.make_async_remote_copy(
                src_ref=ref, dst_ref=ref,
                send_sem=st_send.at[n, slot], recv_sem=st_recv.at[px, slot],
                device_id={"px": lax.rem(px + n, blocks)}, device_id_type=MESH,
            ).start()

    def edge_stat(tile, _):
        for n, (mean, squares) in enumerate(sums(edges, tile)):
            stat_edge[px, tile, 0, n] = mean
            stat_edge[px, tile, 1, n] = squares
        send_stat(stat_edge.at[px, tile], 1 + tile)
        return 0

    for step in range(STEPS):
        now, other = step % 2, (step + 1) % 2
        sides(step, "arrived")
        if step >= 1:
            sides(step - 1, "sent")

        which = range(planes)
        if step == STEPS - 1:
            which = edges
            if planes > 2:
                def middle(tile, _):
                    def row(i, _):
                        update(STEPS - 1, range(1, planes - 1), i, tile)
                        return 0

                    lax.fori_loop(0, lines, row, 0, unroll=4)
                    for n, (mean, squares) in enumerate(sums(range(1, planes - 1), tile)):
                        stat_in[px, 0, n, cells(0, tile), :] = mean
                        stat_in[px, 1, n, cells(0, tile), :] = squares
                    return 0

                lax.fori_loop(0, tiles, middle, 0)
                send_stat(stat_in.at[px], 0)

        def chunk(c, _, step=step, which=which):
            arrived_py(step, c)
            if step >= 1:
                sent_py(step - 1, c)
            tile, first_line = c // pieces, (c % pieces) * rows

            def row(r, _):
                update(step, which, first_line + r, tile)
                return 0

            lax.fori_loop(0, rows, row, 0, unroll=4)
            if step < STEPS - 1:
                send_py(step + 1, c)
                forward_late(step + 1, c)
            else:
                @pl.when(c % pieces == pieces - 1)
                def _():
                    edge_stat(tile, 0)
            return 0

        lax.fori_loop(0, chunks, chunk, 0)
        if step < STEPS - 1:
            forward(step + 1, chunks - 1)
            sides(step + 1, "send")

    def settle(c, _):
        sent_py(STEPS - 1, c)
        return 0

    lax.fori_loop(0, chunks, settle, 0)
    sides(STEPS - 1, "sent")
    for slot, (_, _, via) in enumerate(jobs):
        @pl.when(py == via)
        def _(slot=slot):
            for step in range(STEPS):
                for c in range(chunks // 2):
                    done(relay.at[job_slot(slot), step, c], r_send.at[job_slot(slot), step, c])

    def combine(parts):
        mean = parts[0][0]
        for m, _ in parts[1:]:
            mean = mean + m
        mean = mean / blocks
        squares = jnp.zeros_like(mean)
        for m, q in parts:
            off = m - mean
            squares = squares + (q + lines * (off * off))
        return mean, lax.rsqrt(squares / (lines * blocks) + 0.0001)

    def gathered(at, slot):
        for n in range(1, blocks):
            source = lax.rem(px + n, blocks)
            done(at(px), st_send.at[n, slot])
            done(at(source), st_recv.at[source, slot])

    if planes > 2:
        gathered(lambda p: stat_in.at[p], 0)
        for n in range(planes - 2):
            mean_out[1 + n], scale_out[1 + n] = combine([(stat_in[p, 0, n], stat_in[p, 1, n]) for p in range(blocks)])
    for tile in range(tiles):
        gathered(lambda p: stat_edge.at[p, tile], 1 + tile)
        for n, j in enumerate(edges):
            own = pl.ds(tile * PAD, PAD)
            mean_out[j, own, :], scale_out[j, own, :] = combine(
                [(stat_edge[p, tile, 0, n], stat_edge[p, tile, 1, n]) for p in range(blocks)]
            )


def write_kernel(far, mean, scale, anomaly_out, far_out, scaled, sems):
    planes, lines = far.shape[:2]
    halves = sems.shape[2]
    rows = lines // halves
    whole = [(j, pl.ds(h * rows, rows), h) for j in range(planes) for h in range(halves)]
    keep = [pltpu.make_async_copy(far.at[j, at], far_out.at[j, at], sems.at[0, j, h]) for j, at, h in whole]
    copies = [pltpu.make_async_copy(scaled.at[j, at], anomaly_out.at[j, at], sems.at[1, j, h]) for j, at, h in whole]
    for copy in keep:
        copy.start()
    for (j, at, h), copy in zip(whole, copies):
        middle, factor = mean[j], scale[j]

        def row(i, _, j=j, h=h, middle=middle, factor=factor):
            scaled[j, h * rows + i] = (far[j, h * rows + i] - middle) * factor
            return 0

        lax.fori_loop(0, rows, row, 0, unroll=8)
        copy.start()
    for copy in keep + copies:
        copy.wait()


def shards(jobs, axes, field_now, earlier, speed_square):
    planes, lines, depth, levels = shape = field_now.shape
    tiles = depth // PAD
    pieces = 1
    chunks = tiles * pieces
    rows = lines // pieces
    held = max([1] + [[v for _, _, v in jobs].count(via) for _, _, via in jobs])
    blocks = axes["px"]
    dma = pltpu.SemaphoreType.DMA
    f32 = jnp.float32
    middle = max(planes - 2, 1)
    edges = min(planes, 2)
    vmem = pl.BlockSpec(memory_space=pltpu.VMEM)
    anywhere = pl.BlockSpec(memory_space=pl.ANY)
    far, mean, scale = pl.pallas_call(
        functools.partial(steps_kernel, jobs, pieces, axes),
        out_shape=[
            pltpu.VMEM(shape, f32),
            pltpu.VMEM((planes, depth, levels), f32),
            pltpu.VMEM((planes, depth, levels), f32),
        ],
        in_specs=[anywhere] * 3,
        out_specs=[vmem] * 3,
        scratch_shapes=[
            pltpu.VMEM((2, planes, lines + 2, depth + 2 * PAD, levels), f32),
            pltpu.VMEM(shape, f32),
            pltpu.VMEM((2, 2, lines, depth, levels), f32),
            pltpu.VMEM((held, STEPS, chunks // 2, rows, PAD, levels) if jobs else (1, 1, 1, 1, PAD, levels), f32),
            pltpu.VMEM((blocks, 2, middle, depth, levels), f32),
            pltpu.VMEM((blocks, tiles, 2, edges, PAD, levels), f32),
            dma((3,)),
            dma((2, 2, chunks)),
            dma((2, 2, chunks)),
            dma((held, STEPS, chunks // 2)),
            dma((held, STEPS, chunks // 2)),
            dma((2, 2, 2)),
            dma((2, 2, 2)),
            dma((blocks, 1 + tiles)),
            dma((blocks, 1 + tiles)),
        ],
        compiler_params=pltpu.CompilerParams(
            collective_id=0, has_side_effects=True, vmem_limit_bytes=LIMIT,
        ),
    )(field_now, earlier, speed_square)
    anomaly, far = pl.pallas_call(
        write_kernel,
        out_shape=[jax.ShapeDtypeStruct(shape, f32)] * 2,
        in_specs=[vmem] * 3,
        out_specs=[anywhere] * 2,
        scratch_shapes=[pltpu.VMEM(shape, f32), dma((2, planes, 2))],
        compiler_params=pltpu.CompilerParams(vmem_limit_bytes=24 * 2**20),
    )(far, mean, scale)
    return (anomaly, far)


def solution(mesh):
    axes = dict(mesh.shape)
    return jax.shard_map(
        functools.partial(shards, relays(mesh), axes),
        mesh=mesh,
        in_specs=(P("py", "px", "pz", None),) * 3,
        out_specs=(P("py", "px", "pz", None),) * 2,
        check_vma=False,
    )
```

profile of v0, /device:TPU:5, one launch (start us, length us, event | category | flops | bytes accessed | tf_op | source)
XLA Modules:
  0.0 285.4 jit_solution(9623484373162164991)
XLA Ops:
  0.6 278.8 %shard_map.50 = (f32[4,128,32,128]{3,2,1,0:T(8,128)S(1)}, f32[4,32,128]{2,1,0:T(8,128)S(1)}, f32[4,32,128]{2,1,0:T(8,128)S(1)}) custom-call(f32[4,128,32,128]{3,2,1,0:T(8,128)} %f_ref.1, f32[4,128,32,128]{3,2,1,0:T(8,128)} %e_ref.1, f32[4,128,32,128]{3,2,1,0:T(8,128)} %c_ref.1), custom_call_target="tpu_custom_call" | custom-call | tf_op jit(solution)/shard_map/pallas_call | solution.py:406
  279.4 6.0 %shard_map.51 = (f32[4,128,32,128]{3,2,1,0:T(8,128)}, f32[4,128,32,128]{3,2,1,0:T(8,128)}) custom-call(f32[4,128,32,128]{3,2,1,0:T(8,128)S(1)} %get-tuple-element.5.far, f32[4,32,128]{2,1,0:T(8,128)S(1)} %get-tuple-element.6.mean, f32[4,32,128]{2,1,0:T(8,128)S(1)} %get-tuple-element.7.scale), custom_call_target="tpu_custom_call" | custom-call | tf_op jit(solution)/shard_map/pallas_call | solution.py:436
where the time goes:
time: 289 us; the launch traced here: 285 us
  Pallas kernels  285 us (99%)
    pallas_call x1, Pallas kernels, shards(): pl.pallas_call(functools.partial(steps_kernel, jobs, pieces, axes), out_s...  279 us
    pallas_call x1, Pallas kernels, shards(): pl.pallas_call(write_kernel, out_shape=[jax.ShapeDtypeStruct(shape, f32)]...  5.96 us

commit v1 on v0

--- a/solution.py
+++ b/solution.py
@@ -81,7 +81,7 @@
             for slot, (a, b, via) in enumerate(jobs):
                 if b - a != 2 * way - 1:
                     continue
-                turned = jnp.logical_and(py == a, c % 2 == 1)
+                turned = jnp.logical_and(py == a, c % 2 == 0)
                 direct = jnp.logical_and(direct, jnp.logical_not(turned))
 
                 @pl.when(turned)
@@ -124,7 +124,7 @@
 
     def forward_late(step, c):
         if jobs:
-            @pl.when(jnp.logical_and(c % 2 == 0, c > 0))
+            @pl.when(c % 2 == 1)
             def _():
                 forward(step, c - 1)
 
@@ -191,7 +191,6 @@
     for load in loads:
         load.start()
     lax.fori_loop(2, chunks, first, 0)
-    forward(0, chunks - 1)
 
     for way in (0, 1):
         @pl.when(jnp.logical_not(there("py", way)))
@@ -311,8 +310,8 @@
 
             lax.fori_loop(0, rows, row, 0, unroll=4)
             if step < STEPS - 1:
+                forward_late(step + 1, c)
                 send_py(step + 1, c)
-                forward_late(step + 1, c)
             else:
                 @pl.when(c % pieces == pieces - 1)
                 def _():
@@ -321,7 +320,6 @@
 
         lax.fori_loop(0, chunks, chunk, 0)
         if step < STEPS - 1:
-            forward(step + 1, chunks - 1)
             sides(step + 1, "send")
 
     def settle(c, _):

time: 289 us -> 287 us (level)
  no operation moved by 1% of the time
where the time goes in v1:
time: 287 us; the launch traced here: 285 us
  Pallas kernels  285 us (99%)
    pallas_call x1, Pallas kernels, shards(): pl.pallas_call(functools.partial(steps_kernel, jobs, pieces, axes), out_s...  279 us
    pallas_call x1, Pallas kernels, shards(): pl.pallas_call(write_kernel, out_shape=[jax.ShapeDtypeStruct(shape, f32)]...  5.96 us

profile of v1, /device:TPU:5, one launch (start us, length us, event | category | flops | bytes accessed | tf_op | source)
XLA Modules:
  0.0 285.4 jit_solution(6094184164874967685)
XLA Ops:
  0.6 278.8 %shard_map.50 = (f32[4,128,32,128]{3,2,1,0:T(8,128)S(1)}, f32[4,32,128]{2,1,0:T(8,128)S(1)}, f32[4,32,128]{2,1,0:T(8,128)S(1)}) custom-call(f32[4,128,32,128]{3,2,1,0:T(8,128)} %f_ref.1, f32[4,128,32,128]{3,2,1,0:T(8,128)} %e_ref.1, f32[4,128,32,128]{3,2,1,0:T(8,128)} %c_ref.1), custom_call_target="tpu_custom_call" | custom-call | tf_op jit(solution)/shard_map/pallas_call | solution.py:404
  279.4 6.0 %shard_map.51 = (f32[4,128,32,128]{3,2,1,0:T(8,128)}, f32[4,128,32,128]{3,2,1,0:T(8,128)}) custom-call(f32[4,128,32,128]{3,2,1,0:T(8,128)S(1)} %get-tuple-element.5.far, f32[4,32,128]{2,1,0:T(8,128)S(1)} %get-tuple-element.6.mean, f32[4,32,128]{2,1,0:T(8,128)S(1)} %get-tuple-element.7.scale), custom_call_target="tpu_custom_call" | custom-call | tf_op jit(solution)/shard_map/pallas_call | solution.py:434

commit v2 on v1

--- a/solution.py
+++ b/solution.py
@@ -9,6 +9,7 @@
 
 STEPS = 4
 PAD = 8
+LENT = 5
 LIMIT = 54 * 2**20
 MESH = pl.DeviceIdType.MESH
 
@@ -29,9 +30,18 @@
     return tuple(jobs)
 
 
-def steps_kernel(jobs, pieces, axes, f_ref, e_ref, c_ref, far, mean_out, scale_out,
-                 field, speed, halo, relay, stat_in, stat_edge, load_sem, py_send, py_recv,
-                 r_send, r_recv, side_send, side_recv, st_send, st_recv):
+def paired(mesh):
+    row = mesh.devices[(0,) * (mesh.devices.ndim - 1)]
+    places = [(getattr(device, "coords", None), getattr(device, "core_on_chip", None)) for device in row]
+    if len(places) % 2 or any(None in place for place in places):
+        return False
+    twos = [(places[n], places[n + 1]) for n in range(0, len(places), 2)]
+    return all(tuple(a[0]) == tuple(b[0]) and (a[1], b[1]) == (0, 1) for a, b in twos)
+
+
+def steps_kernel(jobs, pieces, lent, axes, f_ref, e_ref, c_ref, far, mean_out, scale_out,
+                 field, speed, halo, relay, lent_in, stat_in, stat_edge, load_sem, py_send, py_recv,
+                 r_send, r_recv, lent_send, lent_recv, side_send, side_recv, st_send, st_recv):
     planes, lines, depth, levels = c_ref.shape
     tiles = depth // PAD
     chunks = tiles * pieces
@@ -42,16 +52,34 @@
     count = {name: axes[name] for name in axes}
     py = me["py"]
 
+    staged = [
+        pltpu.make_async_copy(f_ref.at[j, :, pl.ds(0, PAD)], far.at[j, :, pl.ds(0, PAD)], load_sem.at[3 + n])
+        for n, j in enumerate(edges)
+    ]
+    for load in staged:
+        load.start()
+
     barrier = pltpu.get_barrier_semaphore()
     greeted = 0
+    met = sorted({(n, n + 1) for n in range(count["py"] - 1)} | {
+        tuple(sorted(pair)) for a, b, via in jobs for pair in ((a, via), (via, b))
+    })
+    for low, high in met:
+        for here, beyond in ((low, high), (high, low)):
+            @pl.when(py == here)
+            def _(beyond=beyond):
+                pl.semaphore_signal(barrier, inc=1, device_id={"py": beyond}, device_id_type=MESH)
+    known = sum((py == here).astype(jnp.int32) for pair in met for here in pair)
     for name in axes:
+        if name == "py":
+            continue
         for n in range(1, count[name]):
             pl.semaphore_signal(
                 barrier, inc=1, device_id={name: lax.rem(me[name] + n, count[name])},
                 device_id_type=MESH,
             )
             greeted += 1
-    pl.semaphore_wait(barrier, greeted)
+    pl.semaphore_wait(barrier, known + greeted)
 
     def there(name, way):
         return me[name] < count[name] - 1 if way else me[name] > 0
@@ -59,20 +87,47 @@
     def done(ref, sem):
         pltpu.make_async_copy(ref, ref, sem).wait()
 
-    def part(c, line, cell):
+    def part(c, line, cell, held=(0, rows)):
         start = cell + (c // pieces) * PAD
         if cell % PAD == 0:
             start = pl.multiple_of(start, PAD)
-        return pl.ds(line + (c % pieces) * rows, rows), pl.ds(start, PAD)
-
-    def edge(step, c, way):
+        return pl.ds(line + (c % pieces) * rows + held[0], held[1]), pl.ds(start, PAD)
+
+    def edge(step, c, way, held=(0, rows)):
         plane = planes - 1 if way else 0
         if step == 0:
-            return f_ref.at[(plane,) + part(c, 0, 0)]
-        return field.at[(step % 2, plane) + part(c, 1, PAD)]
-
-    def landing(step, c, side):
-        return halo.at[(side, step % 2) + part(c, 0, 0)]
+            start = far if isinstance(c, int) else f_ref
+            return start.at[(plane,) + part(c, 0, 0, held)]
+        return field.at[(step % 2, plane) + part(c, 1, PAD, held)]
+
+    def landing(step, c, side, held=(0, rows)):
+        return halo.at[(side, step % 2) + part(c, 0, 0, held)]
+
+    last = STEPS - 1
+    own_part, lent_part = (0, rows - lent), (rows - lent, lent)
+    mate = me["pz"] + 1 - 2 * lax.rem(me["pz"], 2)
+    inner_core = lax.rem(me["pz"], 2) == 0
+
+    def shares(way):
+        busy = there("py", way)
+        for a, b, _ in jobs:
+            if b - a != 2 * way - 1:
+                busy = jnp.logical_and(busy, py != a)
+        return busy
+
+    def pass_lent(c):
+        if lent:
+            for way in (0, 1):
+                @pl.when(jnp.logical_and(jnp.logical_and(c == 2, jnp.logical_not(inner_core)), shares(way)))
+                def _(way=way):
+                    done(lent_in.at[way], lent_recv.at[way])
+                    pltpu.make_async_remote_copy(
+                        src_ref=lent_in.at[way],
+                        dst_ref=landing(last, 1, 1 - way, lent_part),
+                        send_sem=lent_send.at[way],
+                        recv_sem=py_recv.at[1 - way, last % 2, 1],
+                        device_id={"py": py + (2 * way - 1), "pz": mate}, device_id_type=MESH,
+                    ).start()
 
     def send_py(step, c):
         for way in (0, 1):
@@ -81,7 +136,7 @@
             for slot, (a, b, via) in enumerate(jobs):
                 if b - a != 2 * way - 1:
                     continue
-                turned = jnp.logical_and(py == a, c % 2 == 0)
+                turned = jnp.logical_and(py == a, jnp.int32(c) % 2 == 0)
                 direct = jnp.logical_and(direct, jnp.logical_not(turned))
 
                 @pl.when(turned)
@@ -92,6 +147,27 @@
                         send_sem=py_send.at[way, step % 2, c],
                         recv_sem=r_recv.at[job_slot(slot), step, c // 2],
                         device_id={"py": via}, device_id_type=MESH,
+                    ).start()
+
+            if lent and step == last:
+                split = jnp.logical_and(jnp.logical_and(c == 1, inner_core), jnp.logical_and(direct, shares(way)))
+                direct = jnp.logical_and(direct, jnp.logical_not(split))
+
+                @pl.when(split)
+                def _(way=way, beyond=beyond):
+                    pltpu.make_async_remote_copy(
+                        src_ref=edge(step, c, way, lent_part),
+                        dst_ref=lent_in.at[way],
+                        send_sem=py_send.at[way, step % 2, c],
+                        recv_sem=lent_recv.at[way],
+                        device_id={"pz": mate}, device_id_type=MESH,
+                    ).start()
+                    pltpu.make_async_remote_copy(
+                        src_ref=edge(step, c, way, own_part),
+                        dst_ref=landing(step, c, 1 - way, own_part),
+                        send_sem=py_send.at[way, step % 2, c],
+                        recv_sem=py_recv.at[1 - way, step % 2, c],
+                        device_id={"py": beyond}, device_id_type=MESH,
                     ).start()
 
             @pl.when(direct)
@@ -123,7 +199,7 @@
                 ).start()
 
     def forward_late(step, c):
-        if jobs:
+        if jobs and not isinstance(c, int):
             @pl.when(c % 2 == 1)
             def _():
                 forward(step, c - 1)
@@ -186,7 +262,10 @@
         forward_late(0, c)
         return 0
 
-    lax.fori_loop(0, 2, first, 0)
+    for load in staged:
+        load.wait()
+    first(0, 0)
+    first(jnp.int32(1), 0)
     sides(0, "send")
     for load in loads:
         load.start()
@@ -260,12 +339,17 @@
         ]
 
     def send_stat(ref, slot):
-        for n in range(1, blocks):
-            pltpu.make_async_remote_copy(
-                src_ref=ref, dst_ref=ref,
-                send_sem=st_send.at[n, slot], recv_sem=st_recv.at[px, slot],
-                device_id={"px": lax.rem(px + n, blocks)}, device_id_type=MESH,
-            ).start()
+        for n in range(blocks - 1, 0, -1):
+            for way in (0, 1):
+                to = px + n if way else px - n
+
+                @pl.when(to < blocks if way else to >= 0)
+                def _(n=n, way=way, to=to):
+                    pltpu.make_async_remote_copy(
+                        src_ref=ref, dst_ref=ref,
+                        send_sem=st_send.at[n if way else blocks - n, slot], recv_sem=st_recv.at[px, slot],
+                        device_id={"px": to}, device_id_type=MESH,
+                    ).start()
 
     def edge_stat(tile, _):
         for n, (mean, squares) in enumerate(sums(edges, tile)):
@@ -312,6 +396,8 @@
             if step < STEPS - 1:
                 forward_late(step + 1, c)
                 send_py(step + 1, c)
+                if step + 1 == last:
+                    pass_lent(c)
             else:
                 @pl.when(c % pieces == pieces - 1)
                 def _():
@@ -334,6 +420,12 @@
             for step in range(STEPS):
                 for c in range(chunks // 2):
                     done(relay.at[job_slot(slot), step, c], r_send.at[job_slot(slot), step, c])
+
+    if lent:
+        for way in (0, 1):
+            @pl.when(jnp.logical_and(jnp.logical_not(inner_core), shares(way)))
+            def _(way=way):
+                done(lent_in.at[way], lent_send.at[way])
 
     def combine(parts):
         mean = parts[0][0]
@@ -387,12 +479,13 @@
         copy.wait()
 
 
-def shards(jobs, axes, field_now, earlier, speed_square):
+def shards(jobs, pairs, axes, field_now, earlier, speed_square):
     planes, lines, depth, levels = shape = field_now.shape
     tiles = depth // PAD
     pieces = 1
     chunks = tiles * pieces
     rows = lines // pieces
+    lent = rows // LENT if pairs and pieces == 1 and chunks >= 4 else 0
     held = max([1] + [[v for _, _, v in jobs].count(via) for _, _, via in jobs])
     blocks = axes["px"]
     dma = pltpu.SemaphoreType.DMA
@@ -402,7 +495,7 @@
     vmem = pl.BlockSpec(memory_space=pltpu.VMEM)
     anywhere = pl.BlockSpec(memory_space=pl.ANY)
     far, mean, scale = pl.pallas_call(
-        functools.partial(steps_kernel, jobs, pieces, axes),
+        functools.partial(steps_kernel, jobs, pieces, lent, axes),
         out_shape=[
             pltpu.VMEM(shape, f32),
             pltpu.VMEM((planes, depth, levels), f32),
@@ -415,13 +508,16 @@
             pltpu.VMEM(shape, f32),
             pltpu.VMEM((2, 2, lines, depth, levels), f32),
             pltpu.VMEM((held, STEPS, chunks // 2, rows, PAD, levels) if jobs else (1, 1, 1, 1, PAD, levels), f32),
+            pltpu.VMEM((2, max(lent, 1), PAD, levels), f32),
             pltpu.VMEM((blocks, 2, middle, depth, levels), f32),
             pltpu.VMEM((blocks, tiles, 2, edges, PAD, levels), f32),
-            dma((3,)),
+            dma((5,)),
             dma((2, 2, chunks)),
             dma((2, 2, chunks)),
             dma((held, STEPS, chunks // 2)),
             dma((held, STEPS, chunks // 2)),
+            dma((2,)),
+            dma((2,)),
             dma((2, 2, 2)),
             dma((2, 2, 2)),
             dma((blocks, 1 + tiles)),
@@ -445,7 +541,7 @@
 def solution(mesh):
     axes = dict(mesh.shape)
     return jax.shard_map(
-        functools.partial(shards, relays(mesh), axes),
+        functools.partial(shards, relays(mesh), paired(mesh), axes),
         mesh=mesh,
         in_specs=(P("py", "px", "pz", None),) * 3,
         out_specs=(P("py", "px", "pz", None),) * 2,

time: 287 us -> 286 us (level)
  no operation moved by 1% of the time
where the time goes in v2:
time: 286 us
  Pallas kernels  286 us (100%)
    pallas_call x1, Pallas kernels, shards(): pl.pallas_call(functools.partial(steps_kernel, jobs, pieces, lent, axes),...  280 us
    pallas_call x1, Pallas kernels, shards(): pl.pallas_call(write_kernel, out_shape=[jax.ShapeDtypeStruct(shape, f32)]...  5.96 us

profile of v2, /device:TPU:5, one launch (start us, length us, event | category | flops | bytes accessed | tf_op | source)
XLA Modules:
  0.0 286.3 jit_solution(12498749785932755181)
XLA Ops:
  0.6 279.7 %shard_map.50 = (f32[4,128,32,128]{3,2,1,0:T(8,128)S(1)}, f32[4,32,128]{2,1,0:T(8,128)S(1)}, f32[4,32,128]{2,1,0:T(8,128)S(1)}) custom-call(f32[4,128,32,128]{3,2,1,0:T(8,128)} %f_ref.1, f32[4,128,32,128]{3,2,1,0:T(8,128)} %e_ref.1, f32[4,128,32,128]{3,2,1,0:T(8,128)} %c_ref.1), custom_call_target="tpu_custom_call" | custom-call | tf_op jit(solution)/shard_map/pallas_call | solution.py:497
  280.3 6.0 %shard_map.51 = (f32[4,128,32,128]{3,2,1,0:T(8,128)}, f32[4,128,32,128]{3,2,1,0:T(8,128)}) custom-call(f32[4,128,32,128]{3,2,1,0:T(8,128)S(1)} %get-tuple-element.5.far, f32[4,32,128]{2,1,0:T(8,128)S(1)} %get-tuple-element.6.mean, f32[4,32,128]{2,1,0:T(8,128)S(1)} %get-tuple-element.7.scale), custom_call_target="tpu_custom_call" | custom-call | tf_op jit(solution)/shard_map/pallas_call | solution.py:530

commit v3 on v2

--- a/solution.py
+++ b/solution.py
@@ -9,7 +9,7 @@
 
 STEPS = 4
 PAD = 8
-LENT = 5
+LENT = 4
 LIMIT = 54 * 2**20
 MESH = pl.DeviceIdType.MESH
 

time: 286 us -> 286 us (level)
  no operation moved by 1% of the time
where the time goes in v3:
time: 286 us
  Pallas kernels  285 us (100%)
    pallas_call x1, Pallas kernels, shards(): pl.pallas_call(functools.partial(steps_kernel, jobs, pieces, lent, axes),...  279 us
    pallas_call x1, Pallas kernels, shards(): pl.pallas_call(write_kernel, out_shape=[jax.ShapeDtypeStruct(shape, f32)]...  5.96 us

profile of v3, /device:TPU:5, one launch (start us, length us, event | category | flops | bytes accessed | tf_op | source)
XLA Modules:
  0.0 286.1 jit_solution(16259145090864141758)
XLA Ops:
  0.6 279.5 %shard_map.50 = (f32[4,128,32,128]{3,2,1,0:T(8,128)S(1)}, f32[4,32,128]{2,1,0:T(8,128)S(1)}, f32[4,32,128]{2,1,0:T(8,128)S(1)}) custom-call(f32[4,128,32,128]{3,2,1,0:T(8,128)} %f_ref.1, f32[4,128,32,128]{3,2,1,0:T(8,128)} %e_ref.1, f32[4,128,32,128]{3,2,1,0:T(8,128)} %c_ref.1), custom_call_target="tpu_custom_call" | custom-call | tf_op jit(solution)/shard_map/pallas_call | solution.py:497
  280.1 6.0 %shard_map.51 = (f32[4,128,32,128]{3,2,1,0:T(8,128)}, f32[4,128,32,128]{3,2,1,0:T(8,128)}) custom-call(f32[4,128,32,128]{3,2,1,0:T(8,128)S(1)} %get-tuple-element.5.far, f32[4,32,128]{2,1,0:T(8,128)S(1)} %get-tuple-element.6.mean, f32[4,32,128]{2,1,0:T(8,128)S(1)} %get-tuple-element.7.scale), custom_call_target="tpu_custom_call" | custom-call | tf_op jit(solution)/shard_map/pallas_call | solution.py:530

commit v4 on v3

--- a/solution.py
+++ b/solution.py
@@ -10,6 +10,7 @@
 STEPS = 4
 PAD = 8
 LENT = 4
+END = 4
 LIMIT = 54 * 2**20
 MESH = pl.DeviceIdType.MESH
 
@@ -39,9 +40,9 @@
     return all(tuple(a[0]) == tuple(b[0]) and (a[1], b[1]) == (0, 1) for a, b in twos)
 
 
-def steps_kernel(jobs, pieces, lent, axes, f_ref, e_ref, c_ref, far, mean_out, scale_out,
+def steps_kernel(jobs, pieces, lent, end, axes, f_ref, e_ref, c_ref, far, mean_out, scale_out,
                  field, speed, halo, relay, lent_in, stat_in, stat_edge, load_sem, py_send, py_recv,
-                 r_send, r_recv, lent_send, lent_recv, side_send, side_recv, st_send, st_recv):
+                 r_send, r_recv, lent_send, lent_recv, end_recv, side_send, side_recv, st_send, st_recv):
     planes, lines, depth, levels = c_ref.shape
     tiles = depth // PAD
     chunks = tiles * pieces
@@ -105,6 +106,7 @@
 
     last = STEPS - 1
     own_part, lent_part = (0, rows - lent), (rows - lent, lent)
+    head_part, end_part = (0, rows - end), (rows - end, end)
     mate = me["pz"] + 1 - 2 * lax.rem(me["pz"], 2)
     inner_core = lax.rem(me["pz"], 2) == 0
 
@@ -169,6 +171,21 @@
                         recv_sem=py_recv.at[1 - way, step % 2, c],
                         device_id={"py": beyond}, device_id_type=MESH,
                     ).start()
+
+            if end and step == last:
+                ends = jnp.logical_and(direct, c == chunks - 1)
+                direct = jnp.logical_and(direct, c != chunks - 1)
+
+                @pl.when(ends)
+                def _(way=way, beyond=beyond):
+                    for held, sem in ((head_part, py_recv.at[1 - way, step % 2, c]), (end_part, end_recv.at[1 - way])):
+                        pltpu.make_async_remote_copy(
+                            src_ref=edge(step, c, way, held),
+                            dst_ref=landing(step, c, 1 - way, held),
+                            send_sem=py_send.at[way, step % 2, c],
+                            recv_sem=sem,
+                            device_id={"py": beyond}, device_id_type=MESH,
+                        ).start()
 
             @pl.when(direct)
             def _(way=way, beyond=beyond):
@@ -324,7 +341,7 @@
             else:
                 far[j, i, own, :] = later
 
-    def sums(which, tile):
+    def sums(which, tile, held=None, first=0, stop=lines):
         own = cells(0, tile)
         base = [far[j, 0, own, :] for j in which]
 
@@ -333,8 +350,9 @@
             return [(t + m, q + m * m) for (t, q), m in zip(held, moved)]
 
         zero = jnp.zeros((PAD, levels), jnp.float32)
-        held = lax.fori_loop(0, lines, add, [(zero, zero) for _ in which], unroll=8)
-        return [
+        held = [(zero, zero) for _ in which] if held is None else held
+        held = lax.fori_loop(first, stop, add, held, unroll=8)
+        return held if stop < lines else [
             (b + t / lines, jnp.maximum(q - t * (t / lines), 0.0)) for b, (t, q) in zip(base, held)
         ]
 
@@ -351,8 +369,8 @@
                         device_id={"px": to}, device_id_type=MESH,
                     ).start()
 
-    def edge_stat(tile, _):
-        for n, (mean, squares) in enumerate(sums(edges, tile)):
+    def edge_stat(tile, found):
+        for n, (mean, squares) in enumerate(found):
             stat_edge[px, tile, 0, n] = mean
             stat_edge[px, tile, 1, n] = squares
         send_stat(stat_edge.at[px, tile], 1 + tile)
@@ -401,10 +419,27 @@
             else:
                 @pl.when(c % pieces == pieces - 1)
                 def _():
-                    edge_stat(tile, 0)
+                    edge_stat(tile, sums(edges, tile))
             return 0
 
-        lax.fori_loop(0, chunks, chunk, 0)
+        lax.fori_loop(0, chunks - 1 if end and step == last else chunks, chunk, 0)
+        if end and step == last:
+            c, held = chunks - 1, None
+            sent_py(step - 1, c)
+            for first, n in (head_part, end_part):
+                for side in (0, 1):
+                    @pl.when(there("py", side))
+                    def _(side=side, first=first, n=n):
+                        arrival = py_recv.at[side, last % 2, c] if first == 0 else end_recv.at[side]
+                        done(landing(last, c, side, (first, n)), arrival)
+
+                def row(r, _):
+                    update(step, edges, r, c)
+                    return 0
+
+                lax.fori_loop(first, first + n, row, 0, unroll=4)
+                held = sums(edges, c, held, first, first + n)
+            edge_stat(c, held)
         if step < STEPS - 1:
             sides(step + 1, "send")
 
@@ -486,6 +521,7 @@
     chunks = tiles * pieces
     rows = lines // pieces
     lent = rows // LENT if pairs and pieces == 1 and chunks >= 4 else 0
+    end = rows // END if pieces == 1 and chunks >= 4 and (chunks % 2 == 0 or not jobs) else 0
     held = max([1] + [[v for _, _, v in jobs].count(via) for _, _, via in jobs])
     blocks = axes["px"]
     dma = pltpu.SemaphoreType.DMA
@@ -495,7 +531,7 @@
     vmem = pl.BlockSpec(memory_space=pltpu.VMEM)
     anywhere = pl.BlockSpec(memory_space=pl.ANY)
     far, mean, scale = pl.pallas_call(
-        functools.partial(steps_kernel, jobs, pieces, lent, axes),
+        functools.partial(steps_kernel, jobs, pieces, lent, end, axes),
         out_shape=[
             pltpu.VMEM(shape, f32),
             pltpu.VMEM((planes, depth, levels), f32),
@@ -518,6 +554,7 @@
             dma((held, STEPS, chunks // 2)),
             dma((2,)),
             dma((2,)),
+            dma((2,)),
             dma((2, 2, 2)),
             dma((2, 2, 2)),
             dma((blocks, 1 + tiles)),

time: 286 us -> 286 us (level)
  no operation moved by 1% of the time
where the time goes in v4:
time: 286 us; the launch traced here: 285 us
  Pallas kernels  285 us (100%)
    pallas_call x1, Pallas kernels, shards(): pl.pallas_call(functools.partial(steps_kernel, jobs, pieces, lent, end, a...  279 us
    pallas_call x1, Pallas kernels, shards(): pl.pallas_call(write_kernel, out_shape=[jax.ShapeDtypeStruct(shape, f32)]...  5.96 us

profile of v4, /device:TPU:5, one launch (start us, length us, event | category | flops | bytes accessed | tf_op | source)
XLA Modules:
  0.0 285.4 jit_solution(7356659421529172798)
XLA Ops:
  0.6 278.8 %shard_map.50 = (f32[4,128,32,128]{3,2,1,0:T(8,128)S(1)}, f32[4,32,128]{2,1,0:T(8,128)S(1)}, f32[4,32,128]{2,1,0:T(8,128)S(1)}) custom-call(f32[4,128,32,128]{3,2,1,0:T(8,128)} %f_ref.1, f32[4,128,32,128]{3,2,1,0:T(8,128)} %e_ref.1, f32[4,128,32,128]{3,2,1,0:T(8,128)} %c_ref.1), custom_call_target="tpu_custom_call" | custom-call | tf_op jit(solution)/shard_map/pallas_call | solution.py:533
  279.4 6.0 %shard_map.51 = (f32[4,128,32,128]{3,2,1,0:T(8,128)}, f32[4,128,32,128]{3,2,1,0:T(8,128)}) custom-call(f32[4,128,32,128]{3,2,1,0:T(8,128)S(1)} %get-tuple-element.5.far, f32[4,32,128]{2,1,0:T(8,128)S(1)} %get-tuple-element.6.mean, f32[4,32,128]{2,1,0:T(8,128)S(1)} %get-tuple-element.7.scale), custom_call_target="tpu_custom_call" | custom-call | tf_op jit(solution)/shard_map/pallas_call | solution.py:567

commit v5 on v4

--- a/solution.py
+++ b/solution.py
@@ -437,7 +437,7 @@
                     update(step, edges, r, c)
                     return 0
 
-                lax.fori_loop(first, first + n, row, 0, unroll=4)
+                lax.fori_loop(first, first + n, row, 0, unroll=8)
                 held = sums(edges, c, held, first, first + n)
             edge_stat(c, held)
         if step < STEPS - 1:
@@ -569,7 +569,7 @@
         out_shape=[jax.ShapeDtypeStruct(shape, f32)] * 2,
         in_specs=[vmem] * 3,
         out_specs=[anywhere] * 2,
-        scratch_shapes=[pltpu.VMEM(shape, f32), dma((2, planes, 2))],
+        scratch_shapes=[pltpu.VMEM(shape, f32), dma((2, planes, 1))],
         compiler_params=pltpu.CompilerParams(vmem_limit_bytes=24 * 2**20),
     )(far, mean, scale)
     return (anomaly, far)

time: 286 us -> 285 us (level)
  no operation moved by 1% of the time
where the time goes in v5:
time: 285 us
  Pallas kernels  285 us (100%)
    pallas_call x1, Pallas kernels, shards(): pl.pallas_call(functools.partial(steps_kernel, jobs, pieces, lent, end, a...  279 us
    pallas_call x1, Pallas kernels, shards(): pl.pallas_call(write_kernel, out_shape=[jax.ShapeDtypeStruct(shape, f32)]...  5.92 us

profile of v5, /device:TPU:5, one launch (start us, length us, event | category | flops | bytes accessed | tf_op | source)
XLA Modules:
  0.0 285.3 jit_solution(3487935943549510872)
XLA Ops:
  0.6 278.8 %shard_map.50 = (f32[4,128,32,128]{3,2,1,0:T(8,128)S(1)}, f32[4,32,128]{2,1,0:T(8,128)S(1)}, f32[4,32,128]{2,1,0:T(8,128)S(1)}) custom-call(f32[4,128,32,128]{3,2,1,0:T(8,128)} %f_ref.1, f32[4,128,32,128]{3,2,1,0:T(8,128)} %e_ref.1, f32[4,128,32,128]{3,2,1,0:T(8,128)} %c_ref.1), custom_call_target="tpu_custom_call" | custom-call | tf_op jit(solution)/shard_map/pallas_call | solution.py:533
  279.4 5.9 %shard_map.51 = (f32[4,128,32,128]{3,2,1,0:T(8,128)}, f32[4,128,32,128]{3,2,1,0:T(8,128)}) custom-call(f32[4,128,32,128]{3,2,1,0:T(8,128)S(1)} %get-tuple-element.5.far, f32[4,32,128]{2,1,0:T(8,128)S(1)} %get-tuple-element.6.mean, f32[4,32,128]{2,1,0:T(8,128)S(1)} %get-tuple-element.7.scale), custom_call_target="tpu_custom_call" | custom-call | tf_op jit(solution)/shard_map/pallas_call | solution.py:567
